TPU v7x, 128 devices: a whole 4x4x4 slice. The times are simulated.
128 devices in a mesh: dp: 8 (over y, x_hi), expert: 16 (over z, x_lo, core).
Axes of the slice: x: 4 (x_hi: 2, x_lo: 2; x = x_hi * 2 + x_lo), y: 4, z: 4, core: 2. Of those that a mesh axis runs over, the one named last changes fastest.
Arguments:
- expert_ids: int32 [4096, 8], P(('dp', 'expert')), may hold values from 0 to 15, all different within a row; in each aligned block of 32 rows (0 to 31, 32 to 63, ...) at most 20 rows name the same one
- expert_home: int32 [16], replicated, may hold values from 0 to 15, each once
- live_tokens: int32 [128], P(('dp', 'expert')), may hold values from 1 to 32, 3072 in all
- gate_weights: float32 [4096, 8], P(('dp', 'expert')), may hold values from 0.1 to 1
- output_grad: bfloat16 [4096, 7168], P(('dp', 'expert')), may hold values from -6 to 6
- saved_hidden: bfloat16 [4096, 8, 1024], P(('dp', 'expert')), may hold values from -2.5 to 2.5
- down_weight: bfloat16 [16, 1024, 7168], P('expert'), may hold values from -0.1875 to 0.1875
- dense_input: bfloat16 [4096, 7168], P(('dp', 'expert')), may hold values from -24 to 24
- latent_grad: bfloat16 [4096, 256], P(('dp', 'expert')), may hold values from -0.09375 to 0.09375
Outputs:
- hidden_grad: bfloat16 [4096, 8, 1024], P(('dp', 'expert'))
- expert_grad: float32 [16, 1024, 7168], P('expert', 'dp')
- dense_grad: float32 [7168, 256], P(('dp', 'expert'))
Inputs may be any that keep to these rules, and one draw needn't show every extreme that they name: `expert_ids`: each row names 8 different experts. Among the rows of one device no expert is named more than 20 times, and on some devices one expert is named exactly 20 times. A permutation: expert e is held at index expert_home[e] of the expert axis, in every dp replica. `live_tokens`: entry i is the number of real tokens at the start of device i, in the order of the joined dp and expert axes; the rest are padding. Some device has all 32 real.
All inputs are finite; a program needn't handle non-finite values.
Results may differ from a plain program's by a relative error of at most 0.008.
Values may be sent and summed in bfloat16 or wider, within the bound.
A program may use at most 192 MiB of HBM per device.

v0:
```python
import jax
import jax.numpy as jnp
from jax import lax
from jax.sharding import Mesh
from jax.sharding import PartitionSpec as P

DP = ("dp_0", "dp_1")
EXPERT = ("expert_0", "expert_1", "expert_2")
DP_EXPERT = ("dp_0", "dp_1", "expert_0", "expert_1", "expert_2")


def split_up(shard, dim, size):
    dims = shard.shape
    blocks = shard.reshape(*dims[:dim], size, dims[dim] // size, *dims[dim + 1 :])
    return jnp.moveaxis(blocks, dim, 0)


def in_order(blocks, dim):
    blocks = jnp.moveaxis(blocks, 0, dim)
    dims = blocks.shape
    return blocks.reshape(*dims[:dim], dims[dim] * dims[dim + 1], *dims[dim + 2 :])


def moved_by_axis(blocks, axes, sequence):
    inside = blocks.shape[1:]
    result = blocks.reshape(*(lax.axis_size(a) for a in axes), *inside)
    for k in sequence:
        result = lax.all_to_all(result, axes[k], k, k, tiled=True)
    return result.reshape(-1, *inside)


def two_step_exchange(shard, groups, sequence, split_dim, concat_dim):
    size = lax.axis_size(groups[0]) * lax.axis_size(groups[1])
    blocks = split_up(shard, split_dim, size)
    return in_order(moved_by_axis(blocks, groups, sequence), concat_dim)


def side_by_side(arrays, axis, split_dim, concat_dim, along):
    both = jnp.concatenate(arrays, axis=along)
    result, at, gathered = (
        lax.all_to_all(both, axis, split_axis=split_dim, concat_axis=concat_dim, tiled=True),
        0,
        [],
    )
    for a in arrays:
        gathered.append(lax.slice_in_dim(result, at, at + a.shape[along], axis=along))
        at += a.shape[along]
    return tuple(gathered)


def on_device(
    expert_ids,
    expert_home,
    live_tokens,
    gate_weights,
    output_grad,
    saved_hidden,
    down_weight,
    dense_input,
    latent_grad,
):
    n_group = lax.axis_size(EXPERT)
    tok_rows, top_count = expert_ids.shape
    model_width = output_grad.shape[1]
    hidden_units = saved_hidden.shape[2]
    capacity = tok_rows * top_count * 5 // (4 * n_group)
    is_live = jnp.arange(tok_rows, dtype=jnp.int32) < live_tokens[0]
    masked_grad = jnp.where(is_live[:, None], latent_grad, jnp.zeros_like(latent_grad))
    owned_columns = two_step_exchange(
        dense_input, (("dp_0", "dp_1", "expert_0", "expert_1"), "expert_2"), (1, 0), 1, 0
    )
    dense_grad = lax.dot_general(
        owned_columns,
        lax.all_gather(masked_grad, DP_EXPERT, axis=0, tiled=True),
        (((0,), (0,)), ((), ())),
        preferred_element_type=jnp.float32,
    )
    pair_count = tok_rows * top_count
    flat_ids = expert_ids.reshape(pair_count)
    expert_count = expert_home.shape[0]
    id_table = (flat_ids[:, None] == jnp.arange(expert_count, dtype=jnp.int32)[None, :]).astype(
        jnp.int32
    )
    home_slot = jnp.sum(id_table * expert_home[None, :], axis=1)
    slot_table = (home_slot[:, None] == jnp.arange(n_group, dtype=jnp.int32)[None, :]).astype(
        jnp.int32
    )
    earlier = jnp.cumsum(slot_table, axis=0) - slot_table
    position = jnp.sum(earlier * slot_table, axis=1)
    slot_index = home_slot * capacity + position
    pair_ids = jnp.arange(pair_count, dtype=jnp.int32)
    source_pair = jnp.zeros((n_group * capacity,), jnp.int32).at[slot_index].set(pair_ids)
    filled = jnp.zeros((n_group * capacity,), jnp.bool_).at[slot_index].set(True)
    source_token = source_pair // top_count
    pair_scale = (gate_weights * is_live[:, None].astype(jnp.float32)).reshape(pair_count)
    slot_scale = jnp.where(filled, pair_scale[source_pair], jnp.float32(0.0))
    grad_rows = (output_grad[source_token].astype(jnp.float32) * slot_scale[:, None]).astype(
        jnp.bfloat16
    )
    flat_hidden = saved_hidden.reshape(pair_count, hidden_units)
    hidden_rows = jnp.where(filled[:, None], flat_hidden[source_pair], jnp.zeros((), jnp.bfloat16))
    arrived_grad, arrived_hidden = side_by_side(
        (
            grad_rows.reshape(n_group, capacity, model_width),
            hidden_rows.reshape(n_group, capacity, hidden_units),
        ),
        EXPERT,
        0,
        0,
        2,
    )
    arrived_grad = arrived_grad.reshape(n_group * capacity, model_width)
    arrived_hidden = arrived_hidden.reshape(n_group * capacity, hidden_units)
    expert_weight = down_weight[0]
    input_grad = lax.dot_general(
        arrived_grad, expert_weight, (((1,), (1,)), ((), ())), preferred_element_type=jnp.float32
    ).astype(jnp.bfloat16)
    returned = two_step_exchange(
        input_grad.reshape(n_group, capacity, hidden_units),
        (("expert_0", "expert_1"), "expert_2"),
        (1, 0),
        0,
        0,
    )
    expert_grad = lax.psum_scatter(
        lax.dot_general(
            arrived_hidden,
            arrived_grad,
            (((0,), (0,)), ((), ())),
            preferred_element_type=jnp.float32,
        ),
        DP,
        scatter_dimension=0,
        tiled=True,
    )
    hidden_grad = returned.reshape(n_group * capacity, hidden_units)[slot_index].reshape(
        tok_rows, top_count, hidden_units
    )
    return (hidden_grad, expert_grad[None], dense_grad)


def solution(mesh):
    torus = Mesh(
        mesh.devices.reshape(4, 2, 4, 2, 2), ("dp_0", "dp_1", "expert_0", "expert_1", "expert_2")
    )
    in_specs = (
        P(DP_EXPERT, None),
        P(),
        P(DP_EXPERT),
        P(DP_EXPERT, None),
        P(DP_EXPERT, None),
        P(DP_EXPERT, None, None),
        P(EXPERT, None, None),
        P(DP_EXPERT, None),
        P(DP_EXPERT, None),
    )
    out_specs = (P(DP_EXPERT, None, None), P(EXPERT, DP, None), P(DP_EXPERT, None))
    return jax.shard_map(
        on_device, mesh=torus, in_specs=in_specs, out_specs=out_specs, check_vma=False
    )
```

profile of v0, /device:TPU:2, one launch (start us, length us, event | category | flops | bytes accessed | tf_op | source)
XLA Modules:
  0.0 501.7 jit_solution(9455983698504204111)
XLA Ops:
  12.1 2.1 gather_fusion.2
  15.9 6.1 %gather_fusion = bf16[320,7168]{1,0:T(8,128)(2,1)} fusion(bf16[32,7168]{1,0:T(8,128)(2,1)S(1)} %copy-done.2, s32[1024]{0:T(1024)S(1)} %get-tuple-element.6), kind=kCustom, calls=%fused_computation | custom fusion | bytes 9176320 | tf_op jit(solution)/shard_map/gather | solution.py:97
  22.1 8.1 %reshape.102 = f32[16,20,7168]{2,1,0:T(8,128)} reshape(bf16[320,7168]{1,0:T(8,128)(2,1)} %gather_fusion) | data formatting | bytes 13762560 | tf_op jit(solution)/shard_map/convert_element_type | solution.py:97
  31.0 2.5 gather_fusion.1
  33.7 5.6 %multiply_convert_fusion = bf16[16,20,7168]{2,1,0:T(8,128)(2,1)S(1)} fusion(f32[16,20,7168]{2,1,0:T(8,128)} %reshape.102, f32[16,20]{1,0:T(8,128)S(1)} %mul.51), kind=kLoop, calls=%fused_computation.9 | loop fusion | flops 4587520 | bytes 13763840 | tf_op jit(solution)/shard_map/convert_element_type | solution.py:97
  39.3 3.3 pad_maximum_fusion
  42.7 6.9 %all-to-all-start = ((bf16[16,20,8192]{2,1,0:T(8,128)(2,1)}), bf16[16,20,8192]{2,1,0:T(8,128)(2,1)}, u32[]{:S(2)}, u32[]{:S(2)}) async-start(bf16[16,20,8192]{2,1,0:T(8,128)(2,1)} %pad_maximum_fusion), calls=%async_computation | async-start | bytes 12582912 | tf_op jit(solution)/shard_map/all_to_all | solution.py:41
  50.6 70.7 %all-to-all-done = bf16[16,20,8192]{2,1,0:T(8,128)(2,1)} async-done(((bf16[16,20,8192]{2,1,0:T(8,128)(2,1)}), bf16[16,20,8192]{2,1,0:T(8,128)(2,1)}, u32[]{:S(2)}, u32[]{:S(2)}) %all-to-all-start) | async-done | bytes 5242912 | tf_op jit(solution)/shard_map/all_to_all | solution.py:41
  121.3 15.7 %convolution_bitcast_fusion = f32[1024,7168]{1,0:T(8,128)} fusion(bf16[16,20,8192]{2,1,0:T(8,128)(2,1)} %all-to-all-done), kind=kOutput, calls=%fused_computation.6 | convolution fusion | flops 4697620480 | bytes 34603008 | tf_op jit(solution)/shard_map/dot_general | solution.py:126
  138.0 2.1 reshape.100
  141.8 4.1 all_to_all.25
  146.5 1.7 copy.31
  148.2 2.6 reshape.162
  150.8 5.3 %slice.25 = bf16[16,20,7168]{2,1,0:T(8,128)(2,1)} slice(bf16[16,20,8192]{2,1,0:T(8,128)(2,1)} %all-to-all-done), slice={[0:16], [0:20], [0:7168]} | slice | bytes 9175040 | tf_op jit(solution)/shard_map/slice | solution.py:46
  156.2 7.3 %reshape.98 = bf16[320,7168]{1,0:T(8,128)(2,1)} reshape(bf16[16,20,7168]{2,1,0:T(8,128)(2,1)} %slice.25) | data formatting | bytes 9175040 | tf_op jit(solution)/shard_map/reshape | solution.py:112
  163.5 11.6 %fusion.2 = bf16[320,1024]{1,0:T(8,128)(2,1)S(1)} fusion(bf16[320,7168]{1,0:T(8,128)(2,1)} %reshape.98, bf16[1,1024,7168]{2,1,0:T(8,128)(2,1)} %param.15), kind=kOutput, calls=%fused_computation.11 | convolution fusion | flops 4697948160 | bytes 19922944 | tf_op jit(solution)/shard_map/dot_general | solution.py:115
  175.6 4.3 all_to_all.26
  179.9 11.8 %all-to-all-start.4 = ((bf16[64,2,1792]{2,1,0:T(2,128)(2,1)}), bf16[64,2,1792]{2,1,0:T(2,128)(2,1)S(1)}, u32[]{:S(2)}, u32[]{:S(2)}) async-start(bf16[64,2,1792]{2,1,0:T(2,128)(2,1)} %reshape.162), calls=%async_computation.5 | async-start | bytes 917504 | tf_op jit(solution)/shard_map/all_to_all | solution.py:28
  193.2 15.3 %all-to-all-done.4 = bf16[64,2,1792]{2,1,0:T(2,128)(2,1)S(1)} async-done(((bf16[64,2,1792]{2,1,0:T(2,128)(2,1)}), bf16[64,2,1792]{2,1,0:T(2,128)(2,1)S(1)}, u32[]{:S(2)}, u32[]{:S(2)}) %all-to-all-start.4) | async-done | bytes 458784 | tf_op jit(solution)/shard_map/all_to_all | solution.py:28
  208.6 4.3 all-to-all-start.2
  212.9 1.9 reshape.163
  214.8 274.4 %all-gather.2.cloned.1.call-done = bf16[4096,256]{1,0:T(8,128)(2,1)} async-done(((bf16[32,256]{1,0:T(8,128)(2,1)}), bf16[4096,256]{1,0:T(8,128)(2,1)}) %all-gather.2.cloned.1.call-update) | async-done | bytes 2097168 | tf_op jit(solution)/shard_map/all_gather | solution.py:74
  489.2 2.7 convolution_bitcast_fusion.1
  492.2 2.0 gather_fusion.3
  (55 shorter events, 12.8 us)
Async XLA Ops:
  8.0 4.1 copy-start
  8.0 7.9 %copy-start.2 = (bf16[32,7168]{1,0:T(8,128)(2,1)S(1)}, bf16[32,7168]{1,0:T(8,128)(2,1)}, u32[]{:S(2)}) copy-start(bf16[32,7168]{1,0:T(8,128)(2,1)} %param.13) | copy-start | bytes 1376260
  22.1 8.7 %copy-start.5 = (f32[32,8]{0,1:T(8,128)S(1)}, f32[32,8]{0,1:T(8,128)}, u32[]{:S(2)}) copy-start(f32[32,8]{0,1:T(8,128)} %param.12) | copy-start | bytes 3076
  42.7 7.0 %copy-start.4 = (bf16[32,256]{1,0:T(8,128)(2,1)S(1)}, bf16[32,256]{1,0:T(8,128)(2,1)}, u32[]{:S(2)}) copy-start(bf16[32,256]{1,0:T(8,128)(2,1)} %param.17) | copy-start | bytes 49156
  42.7 78.6 %all-to-all-start = ((bf16[16,20,8192]{2,1,0:T(8,128)(2,1)}), bf16[16,20,8192]{2,1,0:T(8,128)(2,1)}, u32[]{:S(2)}, u32[]{:S(2)}) async-start(bf16[16,20,8192]{2,1,0:T(8,128)(2,1)} %pad_maximum_fusion), calls=%async_computation | async-start | bytes 12582912 | tf_op jit(solution)/shard_map/all_to_all | solution.py:41
  49.6 439.6 %all-gather.2.cloned.1.call-start = ((), (), s32[]{:S(2)}) async-start(), calls=%async_computation.7 | async-start | bytes 2113536 | tf_op jit(solution)/shard_map/all_gather | solution.py:74
  50.4 443.8 %reduce-scatter.2.cloned.1.call-start = ((), (), s32[]{:S(2)}) async-start(), calls=%async_computation.6 | async-start | bytes 33030144 | tf_op jit(solution)/shard_map/reduce_scatter | solution.py:125
  137.0 1.0 copy-start.3
  179.9 28.7 %all-to-all-start.4 = ((bf16[64,2,1792]{2,1,0:T(2,128)(2,1)}), bf16[64,2,1792]{2,1,0:T(2,128)(2,1)S(1)}, u32[]{:S(2)}, u32[]{:S(2)}) async-start(bf16[64,2,1792]{2,1,0:T(2,128)(2,1)} %reshape.162), calls=%async_computation.5 | async-start | bytes 917504 | tf_op jit(solution)/shard_map/all_to_all | solution.py:28
  208.6 283.4 %all-to-all-start.2 = ((bf16[8,2,1,20,1024]{4,1,3,2,0:T(2,128)(2,1)}), bf16[8,2,1,20,1024]{4,1,3,2,0:T(2,128)(2,1)S(1)}, u32[]{:S(2)}, u32[]{:S(2)}) async-start(bf16[8,2,1,20,1024]{4,1,3,2,0:T(2,128)(2,1)} %copy.28), calls=%async_computation.2 | async-start | bytes 1310720 | tf_op jit(solution)/shard_map/all_to_all | solution.py:28
  212.9 281.3 %copy-start.1 = (bf16[32,8,1024]{2,1,0:T(8,128)(2,1)S(1)}, bf16[32,8,1024]{2,1,0:T(8,128)(2,1)}, u32[]{:S(2)}) copy-start(bf16[32,8,1024]{2,1,0:T(8,128)(2,1)} %param.14) | copy-start | bytes 1572868
Sparse Core Ops, SparseCore 0:
  52.7 436.4 all-gather.1
Sparse Core Ops, SparseCore 1:
  137.1 311.5 reduce-scatter.1
where the time goes:
time: 503 us; the launch traced here: 502 us
  waiting for transfers between devices  360 us (72%)
  local copies, waits for them, and re-layouts  51.8 us (10%)
  matrix products  30 us (6%)
  starting transfers between devices  23.3 us (5%)
  between operations  16.4 us (3%)
  other arithmetic  11.3 us (2%)
  blocking collectives  8.38 us (2%)
    all_gather x1, waiting for transfers between devices, on_device(): lax.all_gather(masked_grad, DP_EXPERT, axis=0, tiled=True)  274 us
    all_to_all x1, waiting for transfers between devices, side_by_side(): lax.all_to_all(both, axis, split_axis=split_dim, concat_axis=concat_dim,...  70.7 us
    all_to_all x2, starting transfers between devices, moved_by_axis(): result = lax.all_to_all(result, axes[k], k, k, tiled=True)  16.1 us
    dot_general x1, matrix products, on_device(): lax.dot_general(arrived_hidden, arrived_grad, (((0,), (0,)), ((), ())), p...  15.7 us
    all_to_all x2, waiting for transfers between devices, moved_by_axis(): result = lax.all_to_all(result, axes[k], k, k, tiled=True)  15.3 us
    dot_general x1, matrix products, on_device(): lax.dot_general(arrived_grad, expert_weight, (((1,), (1,)), ((), ())), pr...  11.6 us
  transfers between devices with their start and end apart: 5, of which 3 were waited for; matrix products, arithmetic and copies ran while one was open for 12% of the time, Pallas kernels for 0%

commit v1 on v0

--- a/solution.py
+++ b/solution.py
@@ -71,7 +71,10 @@
     )
     dense_grad = lax.dot_general(
         owned_columns,
-        lax.all_gather(masked_grad, DP_EXPERT, axis=0, tiled=True),
+        jnp.concatenate(
+            lax.all_to_all(jnp.stack([masked_grad] * lax.axis_size(DP_EXPERT)), DP_EXPERT, 0, 0),
+            axis=0,
+        ),
         (((0,), (0,)), ((), ())),
         preferred_element_type=jnp.float32,
     )

time: 503 us -> 477 us (0.948)
  waiting for transfers between devices: 360 us -> 250 us
  blocking collectives: 8.38 us -> 86.4 us
  local copies, waits for them, and re-layouts: 51.8 us -> 58.3 us
    all_gather x1 -> x0, waiting for transfers between devices: 274 us -> none  [on_device(): lax.all_gather(masked_grad, DP_EXPERT, axis=0, tiled=True)]
    reduce_scatter x1, waiting for transfers between devices: 0.01 us -> 211 us  [on_device(): lax.psum_scatter(lax.dot_general(arrived_hidden, arrived_grad, (((0,), (0...]
    all_to_all x0 -> x1, blocking collectives: none -> 78.1 us  [side_by_side(): lax.all_to_all(both, axis, split_axis=split_dim, concat_axis=concat_dim,...]
    all_to_all x1, waiting for transfers between devices: 70.7 us -> 30.5 us  [on_device(): lax.all_to_all(jnp.stack([masked_grad] * lax.axis_size(DP_EXPERT)), DP_EX...]
    all_to_all x2, waiting for transfers between devices: 15.3 us -> 8.7 us  [moved_by_axis(): result = lax.all_to_all(result, axes[k], k, k, tiled=True)]
    unnamed x17 -> x21, local copies, waits for them, and re-layouts: 7.81 us -> 12.7 us
  transfers between devices with their start and end apart: 5 -> 4, of which waited for: 3 -> 3; matrix products, arithmetic and copies ran while one was open for 12% -> 10% of each run, Pallas kernels for 0% -> 0%
where the time goes in v1:
time: 477 us; the launch traced here: 475 us
  waiting for transfers between devices  250 us (52%)
  blocking collectives  86.4 us (18%)
  local copies, waits for them, and re-layouts  58.3 us (12%)
  matrix products  28.2 us (6%)
  starting transfers between devices  23.7 us (5%)
  between operations  15 us (3%)
  other arithmetic  12.9 us (3%)
    reduce_scatter x1, waiting for transfers between devices, on_device(): lax.psum_scatter(lax.dot_general(arrived_hidden, arrived_grad, (((0,), (0...  211 us
    all_to_all x1, blocking collectives, side_by_side(): lax.all_to_all(both, axis, split_axis=split_dim, concat_axis=concat_dim,...  78.1 us
    all_to_all x1, waiting for transfers between devices, on_device(): lax.all_to_all(jnp.stack([masked_grad] * lax.axis_size(DP_EXPERT)), DP_EX...  30.5 us
    all_to_all x2, starting transfers between devices, moved_by_axis(): result = lax.all_to_all(result, axes[k], k, k, tiled=True)  14.3 us
    dot_general x1, matrix products, on_device(): lax.dot_general(arrived_hidden, arrived_grad, (((0,), (0,)), ((), ())), p...  13.7 us
    unnamed x21, local copies, waits for them, and re-layouts  12.7 us
    dot_general x1, matrix products, on_device(): lax.dot_general(arrived_grad, expert_weight, (((1,), (1,)), ((), ())), pr...  12 us
  transfers between devices with their start and end apart: 4, of which 3 were waited for; matrix products, arithmetic and copies ran while one was open for 10% of the time, Pallas kernels for 0%

profile of v1, /device:TPU:2, one launch (start us, length us, event | category | flops | bytes accessed | tf_op | source)
XLA Modules:
  0.0 475.0 jit_solution(10283012527739235197)
XLA Ops:
  11.3 2.1 gather_fusion.2
  15.1 6.1 %gather_fusion = bf16[320,7168]{1,0:T(8,128)(2,1)} fusion(bf16[32,7168]{1,0:T(8,128)(2,1)S(1)} %copy-done.2, s32[1024]{0:T(1024)S(1)} %get-tuple-element.6), kind=kCustom, calls=%fused_computation | custom fusion | bytes 9176320 | tf_op jit(solution)/shard_map/gather | solution.py:100
  21.3 8.1 %reshape.108 = f32[16,20,7168]{2,1,0:T(8,128)} reshape(bf16[320,7168]{1,0:T(8,128)(2,1)} %gather_fusion) | data formatting | bytes 13762560 | tf_op jit(solution)/shard_map/convert_element_type | solution.py:100
  30.2 2.5 gather_fusion.1
  32.9 8.0 %multiply_convert_fusion = bf16[16,20,7168]{2,1,0:T(8,128)(2,1)} fusion(f32[16,20,7168]{2,1,0:T(8,128)} %reshape.108, f32[16,20]{1,0:T(8,128)S(1)} %mul.51), kind=kLoop, calls=%fused_computation.9 | loop fusion | flops 4587520 | bytes 13763840 | tf_op jit(solution)/shard_map/convert_element_type | solution.py:100
  40.9 3.3 pad_maximum_fusion
  44.2 78.1 %all_to_all.30 = bf16[16,20,8192]{2,1,0:T(8,128)(2,1)S(1)} all-to-all(bf16[16,20,8192]{2,1,0:T(8,128)(2,1)S(1)} %pad_maximum_fusion), channel_id=1, replica_groups=mesh['dp_0'=4,'dp_1'=2,'expert_0'=4,'expert_1'=2,'expert_2'=2] {'expert_..., dimensions={0} | all-to-all | bytes 10485760 | tf_op jit(solution)/shard_map/all_to_all | solution.py:41
  122.2 2.6 copy-done.3
  124.9 13.7 %convolution_bitcast_fusion = f32[1024,7168]{1,0:T(8,128)} fusion(bf16[16,20,8192]{2,1,0:T(8,128)(2,1)S(1)} %all_to_all.30), kind=kOutput, calls=%fused_computation.6 | convolution fusion | flops 4697620480 | bytes 34603008 | tf_op jit(solution)/shard_map/dot_general | solution.py:129
  139.6 2.1 reshape.106
  143.4 4.1 all_to_all.31
  149.8 2.6 reshape.168
  152.4 8.7 %all-to-all-start.5 = ((bf16[64,2,1792]{2,1,0:T(2,128)(2,1)}), bf16[64,2,1792]{2,1,0:T(2,128)(2,1)S(1)}, u32[]{:S(2)}, u32[]{:S(2)}) async-start(bf16[64,2,1792]{2,1,0:T(2,128)(2,1)} %reshape.168), calls=%async_computation.6 | async-start | bytes 917504 | tf_op jit(solution)/shard_map/all_to_all | solution.py:28
  161.2 5.4 %slice.25 = bf16[16,20,7168]{2,1,0:T(8,128)(2,1)} slice(bf16[16,20,8192]{2,1,0:T(8,128)(2,1)} %copy-done.3), slice={[0:16], [0:20], [0:7168]} | slice | bytes 9175040 | tf_op jit(solution)/shard_map/slice | solution.py:46
  166.6 7.3 %reshape.103 = bf16[320,7168]{1,0:T(8,128)(2,1)} reshape(bf16[16,20,7168]{2,1,0:T(8,128)(2,1)} %slice.25) | data formatting | bytes 9175040 | tf_op jit(solution)/shard_map/reshape | solution.py:115
  174.0 12.0 %fusion.2 = bf16[320,1024]{1,0:T(8,128)(2,1)S(1)} fusion(bf16[320,7168]{1,0:T(8,128)(2,1)} %reshape.103, bf16[1,1024,7168]{2,1,0:T(8,128)(2,1)} %param.15), kind=kOutput, calls=%fused_computation.11 | convolution fusion | flops 4697948160 | bytes 19922944 | tf_op jit(solution)/shard_map/dot_general | solution.py:118
  186.5 4.3 all_to_all.32
  192.4 9.4 %all-to-all-start.3 = ((bf16[128,32,256]{2,1,0:T(8,128)(2,1)}), bf16[128,32,256]{2,1,0:T(8,128)(2,1)S(1)}, u32[]{:S(2)}, u32[]{:S(2)}) async-start(bf16[128,32,256]{2,1,0:T(8,128)(2,1)} %stack.2), calls=%async_computation.4 | async-start | bytes 4194304 | tf_op jit(solution)/shard_map/all_to_all | solution.py:75
  203.3 30.5 %all-to-all-done.3 = bf16[128,32,256]{2,1,0:T(8,128)(2,1)S(1)} async-done(((bf16[128,32,256]{2,1,0:T(8,128)(2,1)}), bf16[128,32,256]{2,1,0:T(8,128)(2,1)S(1)}, u32[]{:S(2)}, u32[]{:S(2)}) %all-to-all-start.3) | async-done | bytes 2097184 | tf_op jit(solution)/shard_map/all_to_all | solution.py:75
  233.8 5.6 %all-to-all-start.2 = ((bf16[8,2,1,20,1024]{4,1,3,2,0:T(2,128)(2,1)}), bf16[8,2,1,20,1024]{4,1,3,2,0:T(2,128)(2,1)S(1)}, u32[]{:S(2)}, u32[]{:S(2)}) async-start(bf16[8,2,1,20,1024]{4,1,3,2,0:T(2,128)(2,1)} %copy.28), calls=%async_computation.2 | async-start | bytes 1310720 | tf_op jit(solution)/shard_map/all_to_all | solution.py:28
  239.4 4.1 reshape.169
  243.5 2.4 convolution_bitcast_fusion.1
  246.0 8.7 %all-to-all-done.2 = bf16[8,2,1,20,1024]{4,1,3,2,0:T(2,128)(2,1)S(1)} async-done(((bf16[8,2,1,20,1024]{4,1,3,2,0:T(2,128)(2,1)}), bf16[8,2,1,20,1024]{4,1,3,2,0:T(2,128)(2,1)S(1)}, u32[]{:S(2)}, u32[]{:S(2)}) %all-to-all-start.2) | async-done | bytes 655392 | tf_op jit(solution)/shard_map/all_to_all | solution.py:28
  256.9 211.2 %reduce-scatter.2.cloned.1.call-done = f32[128,7168]{1,0:T(8,128)} async-done(((f32[1024,7168]{1,0:T(8,128)}), f32[128,7168]{1,0:T(8,128)}) %reduce-scatter.2.cloned.1.call-update) | async-done | bytes 3670032 | tf_op jit(solution)/shard_map/reduce_scatter | solution.py:128
  (57 shorter events, 17.1 us)
Async XLA Ops:
  7.2 4.1 copy-start
  7.2 8.0 %copy-start.2 = (bf16[32,7168]{1,0:T(8,128)(2,1)S(1)}, bf16[32,7168]{1,0:T(8,128)(2,1)}, u32[]{:S(2)}) copy-start(bf16[32,7168]{1,0:T(8,128)(2,1)} %param.13) | copy-start | bytes 1376260
  7.2 461.0 %reduce-scatter.2.cloned.1.call-start = ((), (), s32[]{:S(2)}) async-start(), calls=%async_computation.7 | async-start | bytes 33030144 | tf_op jit(solution)/shard_map/reduce_scatter | solution.py:128
  21.3 8.7 %copy-start.7 = (f32[32,8]{0,1:T(8,128)S(1)}, f32[32,8]{0,1:T(8,128)}, u32[]{:S(2)}) copy-start(f32[32,8]{0,1:T(8,128)} %param.12) | copy-start | bytes 3076
  122.2 2.6 copy-start.3
  138.6 1.0 copy-start.5
  139.6 21.6 %copy-start.6 = (bf16[32,256]{1,0:T(8,128)(2,1)S(1)}, bf16[32,256]{1,0:T(8,128)(2,1)}, u32[]{:S(2)}) copy-start(bf16[32,256]{1,0:T(8,128)(2,1)} %param.17) | copy-start | bytes 49156
  152.4 34.1 %all-to-all-start.5 = ((bf16[64,2,1792]{2,1,0:T(2,128)(2,1)}), bf16[64,2,1792]{2,1,0:T(2,128)(2,1)S(1)}, u32[]{:S(2)}, u32[]{:S(2)}) async-start(bf16[64,2,1792]{2,1,0:T(2,128)(2,1)} %reshape.168), calls=%async_computation.6 | async-start | bytes 917504 | tf_op jit(solution)/shard_map/all_to_all | solution.py:28
  186.5 47.3 %copy-start.4 = (bf16[64,2,1792]{2,1,0:T(2,128)(2,1)}, bf16[64,2,1792]{2,1,0:T(2,128)(2,1)S(1)}, u32[]{:S(2)}) copy-start(bf16[64,2,1792]{2,1,0:T(2,128)(2,1)S(1)} %all-to-all-done.5) | copy-start | bytes 1376260
  192.4 41.4 %all-to-all-start.3 = ((bf16[128,32,256]{2,1,0:T(8,128)(2,1)}), bf16[128,32,256]{2,1,0:T(8,128)(2,1)S(1)}, u32[]{:S(2)}, u32[]{:S(2)}) async-start(bf16[128,32,256]{2,1,0:T(8,128)(2,1)} %stack.2), calls=%async_computation.4 | async-start | bytes 4194304 | tf_op jit(solution)/shard_map/all_to_all | solution.py:75
  233.8 20.8 %all-to-all-start.2 = ((bf16[8,2,1,20,1024]{4,1,3,2,0:T(2,128)(2,1)}), bf16[8,2,1,20,1024]{4,1,3,2,0:T(2,128)(2,1)S(1)}, u32[]{:S(2)}, u32[]{:S(2)}) async-start(bf16[8,2,1,20,1024]{4,1,3,2,0:T(2,128)(2,1)} %copy.28), calls=%async_computation.2 | async-start | bytes 1310720 | tf_op jit(solution)/shard_map/all_to_all | solution.py:28
  239.4 228.7 %copy-start.1 = (bf16[32,8,1024]{2,1,0:T(8,128)(2,1)S(1)}, bf16[32,8,1024]{2,1,0:T(8,128)(2,1)}, u32[]{:S(2)}) copy-start(bf16[32,8,1024]{2,1,0:T(8,128)(2,1)} %param.14) | copy-start | bytes 1572868
Sparse Core Ops, SparseCore 0:
  138.7 329.3 reduce-scatter.1
